TPU v7x, 32 devices: a whole 2x2x4 slice. The times are simulated.
32 devices in a mesh: seq: 8 (over z, x), tp: 4 (over y, core).
Axes of the slice: x: 2, y: 2, z: 4, core: 2. Of those that a mesh axis runs over, the one named last changes fastest.
Arguments:
- layer_in: bfloat16 [6144, 2048], P('seq', 'tp'), may hold values from -6 to 6
- attn_gain: float32 [2048], replicated, may hold values from 0.1 to 1.9
- qkv_weight: bfloat16 [3, 2048, 1024], P(None, None, 'tp'), may hold values from -0.125 to 0.125
- log_decay: float32 [8, 6144], P('tp', 'seq'), may hold values from -0.1 to 0
- write_rate: float32 [8, 6144], P('tp', 'seq'), may hold values from 0 to 0.9
- head_gain: float32 [128], replicated, may hold values from 0.1 to 1.9
- out_weight: bfloat16 [1024, 2048], P('tp'), may hold values from -0.1875 to 0.1875
- ffn_gain: float32 [2048], replicated, may hold values from 0.1 to 1.9
- gate_weight: bfloat16 [2048, 2560], P(None, 'tp'), may hold values from -0.125 to 0.125
- up_weight: bfloat16 [2048, 2560], P(None, 'tp'), may hold values from -0.125 to 0.125
- down_weight: bfloat16 [2560, 2048], P('tp'), may hold values from -0.125 to 0.125
Outputs:
- layer_out: bfloat16 [6144, 2048], P('seq', 'tp')
All inputs are finite; a program needn't handle non-finite values.
Results may differ from a plain program's by a relative error of at most 0.014.
Values may be sent and summed in bfloat16 or wider, within the bound.
A program may use at most 128 MiB of HBM per device.

v0:
```python
import functools

import jax
import jax.numpy as jnp
from jax import lax
from jax.experimental import pallas as pl
from jax.experimental.pallas import tpu as pltpu
from jax.sharding import PartitionSpec as P

norm_floor = 0.1
head_floor = 0.05
bf16 = jnp.bfloat16
f32 = jnp.float32
MESH = pl.DeviceIdType.MESH


def mm(a, b):
    return jnp.dot(a, b, preferred_element_type=f32)


def mm_nt(a, b):
    return lax.dot_general(a, b, (((1,), (1,)), ((), ())), preferred_element_type=f32)


def mm_tn(a, b):
    return lax.dot_general(a, b, (((0,), (0,)), ((), ())), preferred_element_type=f32)


def split_mm(a, b):
    high = a.astype(bf16)
    low = (a - high.astype(f32)).astype(bf16)
    return mm(high, b) + mm(low, b)


def unit_rows(u):
    return u * lax.rsqrt(jnp.sum(u * u, axis=-1, keepdims=True) + 1.0)


def kernel(
    cfg,
    x_hbm,
    again_ref,
    qkv_hbm,
    decay_ref,
    rate_ref,
    hgain_ref,
    wo_hbm,
    fgain_ref,
    gate_hbm,
    up_hbm,
    down_hbm,
    out_ref,
    x_full,
    qkv_w,
    gate_w,
    up_w,
    down_w,
    wo_full,
    o_buf,
    p_buf,
    heads_all,
    state,
    excl,
    s_send_buf,
    s_recv_buf,
    last_send_buf,
    last_recv_buf,
    res_tmp,
    res_own,
    part_buf,
    rp_buf,
    cs_buf,
    cr_buf,
    out_buf,
    l_sem,
    x_send,
    x_recv,
    w_send,
    w_recv,
    h_send,
    h_recv,
    s_send,
    s_recv,
    rp_send,
    rp_recv,
    rc_send,
    rc_recv,
    g_send,
    g_recv,
    o_sem,
):
    n_tp, n_seq, span, width, steps, group = cfg
    length, cw = x_hbm.shape
    heads = qkv_hbm.shape[2] // width
    hw = heads * width
    half = n_tp // 2
    nc = length // span
    piece = width
    nh = length // piece
    share = hw // group
    subs = span // width
    t = lax.axis_index("tp")
    s = lax.axis_index("seq")
    pt = t + 1 - 2 * lax.rem(t, 2)
    r = lax.rem(s, group)
    base = s - r

    def to_tp(k):
        return lax.rem(t + 2 * k, n_tp)

    def from_tp(k):
        return lax.rem(t + n_tp - 2 * k, n_tp)

    def pair_tp(k):
        return lax.rem(pt + n_tp - 2 * k, n_tp)

    barrier = pltpu.get_barrier_semaphore()
    arrivals = 0
    for other in [pt] + [to_tp(k) for k in range(1, half)] + [from_tp(k) for k in range(1, half)]:
        pl.semaphore_signal(barrier, inc=1, device_id={"tp": other}, device_id_type=MESH)
        arrivals += 1
    for j in range(steps):
        d = 2**j

        @pl.when(s + d < n_seq)
        def _(d=d):
            pl.semaphore_signal(barrier, inc=1, device_id={"seq": s + d}, device_id_type=MESH)

        @pl.when(s >= d)
        def _(d=d):
            pl.semaphore_signal(barrier, inc=1, device_id={"seq": s - d}, device_id_type=MESH)

        arrivals = arrivals + 1 - (s + d) // n_seq + (s + n_seq - d) // n_seq

    for g in range(1, group):
        other = base + lax.rem(r + g, group)
        pl.semaphore_signal(barrier, inc=1, device_id={"seq": other}, device_id_type=MESH)
        arrivals += 1

    def cols(j, w):
        return pl.ds(pl.multiple_of(j * w, w), w)

    def rows(i):
        return pl.ds(pl.multiple_of(i * span, span), span)

    def fine(i):
        return pl.ds(pl.multiple_of(i * piece, piece), piece)

    loads = [
        pltpu.make_async_copy(qkv_hbm, qkv_w, l_sem.at[0]),
        pltpu.make_async_copy(x_hbm, x_full.at[:, cols(t, cw)], l_sem.at[1]),
        pltpu.make_async_copy(wo_hbm, wo_full.at[cols(t, hw), :], l_sem.at[2]),
        pltpu.make_async_copy(gate_hbm, gate_w, l_sem.at[3]),
        pltpu.make_async_copy(up_hbm, up_w, l_sem.at[4]),
        pltpu.make_async_copy(down_hbm, down_w, l_sem.at[5]),
    ]
    for load in loads[:2]:
        load.start()
    pl.semaphore_wait(barrier, arrivals)

    def remote(src, dst, send, recv, axis, other):
        return pltpu.make_async_remote_copy(
            src_ref=src,
            dst_ref=dst,
            send_sem=send,
            recv_sem=recv,
            device_id={axis: other},
            device_id_type=MESH,
        )

    def x_slot(i, who):
        return x_full.at[rows(i), cols(who, cw)]

    def x_copy(slot, i, src, who, other):
        return remote(src, x_slot(i, who), x_send.at[slot, i], x_recv.at[slot, i], "tp", other)

    def h_slot(i, who):
        return heads_all.at[fine(i), cols(who, hw)]

    def h_copy(slot, i, who, other):
        return remote(
            h_slot(i, who), h_slot(i, who), h_send.at[slot, i], h_recv.at[slot, i], "tp", other
        )

    def w_slot(who):
        return wo_full.at[cols(who, hw), :]

    def w_part(who, j):
        return wo_full.at[pl.ds(pl.multiple_of(who * hw + j * share, share), share), :]

    def part_copy(k, who, other):
        src = wo_hbm.at[pl.ds(pl.multiple_of(r * share, share), share), :]
        return remote(src, w_part(who, r), w_send.at[k], w_recv.at[k], "tp", other)

    def group_copy(k, g, j):
        slot = w_part(from_tp(k), j)
        other = base + lax.rem(r + g, group)
        return remote(slot, slot, g_send.at[k - 1, g], g_recv.at[k - 1, g], "seq", other)

    def w_copy(slot, src, who, other):
        return remote(src, w_slot(who), w_send.at[slot], w_recv.at[slot], "tp", other)

    def send_x(i, carry):
        for k in range(1, half):
            x_copy(k, i, x_hbm.at[rows(i), :], t, to_tp(k)).start()
        x_copy(0, i, x_hbm.at[rows(i), :], t, pt).start()

        @pl.when(i == 0)
        def _():
            for k in range(1, half):
                part_copy(k, t, to_tp(k)).start()

        return carry

    lax.fori_loop(0, nc, send_x, 0)
    for load in loads[2:]:
        load.start()
    loads[0].wait()
    loads[1].wait()

    row_id = lax.broadcasted_iota(jnp.int32, (width, width), 0)
    col_id = lax.broadcasted_iota(jnp.int32, (width, width), 1)
    eye = (row_id == col_id).astype(f32)
    upto = (row_id <= col_id).astype(f32)
    for h in range(heads):
        state[h] = jnp.concatenate([eye, jnp.zeros((width, width), f32)], axis=1)

    def stage_one(i, carry):
        for k in range(1, half):
            x_copy(k, i, x_slot(i, from_tp(k)), from_tp(k), pt).wait_recv()
            x_copy(half - 1 + k, i, x_slot(i, from_tp(k)), from_tp(k), pt).start()

        @pl.when(i == 1)
        def _():
            for k in range(1, half):
                part_copy(k, from_tp(k), pt).wait_recv()
                for g in range(1, group):
                    group_copy(k, g, r).start()
            w_copy(0, wo_hbm, t, pt).start()

        x_copy(0, i, x_slot(i, pt), pt, pt).wait_recv()
        for k in range(1, half):
            x_copy(half - 1 + k, i, x_slot(i, pair_tp(k)), pair_tp(k), pt).wait_recv()
        x = x_full[rows(i), :].astype(f32)
        scale = lax.rsqrt(jnp.mean(x * x, axis=1, keepdims=True) + norm_floor)
        normed = (x * scale * again_ref[...]).astype(bf16)
        q_all = mm(normed, qkv_w[0])
        k_all = mm(normed, qkv_w[1])
        v_all = mm(normed, qkv_w[2])
        xor = row_id ^ col_id
        chains = [(c, h) for c in range(subs) for h in range(heads)]
        lower, mixing, right, tail, growth_q, last = {}, {}, {}, {}, {}, {}
        for c in range(subs):
            at = pl.ds(pl.multiple_of(i * span + c * width, width), width)
            cumul = jnp.dot(
                decay_ref[:, at], upto, precision=lax.Precision.HIGHEST, preferred_element_type=f32
            )
            rate = rate_ref[:, at]
            for h in range(heads):
                cell = (c, h)
                part = (slice(c * width, (c + 1) * width), slice(h * width, (h + 1) * width))
                q = unit_rows(q_all[part])
                k = unit_rows(k_all[part])
                v = v_all[part]
                c_row = jnp.broadcast_to(cumul[h : h + 1, :], (width, width))
                c_col = c_row.T
                b_col = jnp.broadcast_to(rate[h : h + 1, :], (width, width)).T
                c_end = cumul[h : h + 1, width - 1 : width]
                weights = jnp.exp(jnp.minimum(c_col - c_row, 0.0))
                growth = jnp.exp(c_col)
                kb = k.astype(bf16)
                both = mm_nt(jnp.concatenate([kb, q.astype(bf16)], axis=0), kb)
                lower[cell] = jnp.where(row_id > col_id, b_col * both[:width] * weights, 0.0)
                mixing[cell] = jnp.where(row_id >= col_id, both[width:] * weights, 0.0).astype(bf16)
                right[cell] = jnp.concatenate([b_col * v, b_col * growth * k], axis=1).astype(bf16)
                tail[cell] = (k * jnp.exp(c_end - c_col)).astype(bf16)
                growth_q[cell] = growth * q
                last[cell] = jnp.exp(c_end)
        inverse = {cell: eye - jnp.where(xor < 2, lower[cell], 0.0) for cell in chains}
        block = 2
        while block < width:
            now = (xor >= block) & (xor < 2 * block)
            small = {cell: inverse[cell].astype(bf16) for cell in chains}
            half_way = {
                cell: mm(small[cell], jnp.where(now, lower[cell], 0.0).astype(bf16))
                for cell in chains
            }
            inverse = {
                cell: inverse[cell] - mm(half_way[cell].astype(bf16), small[cell])
                for cell in chains
            }
            block *= 2
        solved = {cell: mm(inverse[cell].astype(bf16), right[cell]).astype(bf16) for cell in chains}
        mixed = {cell: mm(mixing[cell], solved[cell]) for cell in chains}
        moved = {cell: mm_tn(tail[cell], solved[cell]) for cell in chains}
        for c in range(subs):
            at = pl.ds(pl.multiple_of(i * span + c * width, width), width)
            for h in range(heads):
                cell = (c, h)
                lanes = slice(h * width, (h + 1) * width)
                before = state[h]
                before_b = before.astype(bf16)
                entry = (growth_q[cell] - mixed[cell][:, width:]).astype(bf16)
                entered = mm(entry, before_b)
                p_buf[at, lanes] = entered[:, :width].astype(bf16)
                o_buf[at, lanes] = mixed[cell][:, :width] + entered[:, width:]
                change = mm(moved[cell][:, width:].astype(bf16), before_b)
                after = last[cell] * before - change
                state[h] = jnp.concatenate(
                    [after[:, :width], after[:, width:] + moved[cell][:, :width]], axis=1
                )
        return carry

    lax.fori_loop(0, nc, stage_one, 0)

    def s_copy(j, h):
        src, dst = (s_send_buf.at[j, h], s_recv_buf.at[j, h])
        if j + 1 == steps:
            src, dst = (last_send_buf.at[h], last_recv_buf.at[h])
        return remote(src, dst, s_send.at[j, h], s_recv.at[j, h], "seq", lax.rem(s + 2**j, n_seq))

    for h in range(heads):
        excl[h] = jnp.concatenate([eye, jnp.zeros((width, width), f32)], axis=1)
    for j in range(steps):
        d = 2**j

        @pl.when(s + d < n_seq)
        def _(j=j):
            if j + 1 == steps:
                last_send_buf[...] = state[:, :, width:].astype(bf16)
            else:
                s_send_buf[j] = state[...].astype(bf16)
            for h in range(heads):
                s_copy(j, h).start()

        if j == 0:
            for k in range(1, half):
                for g in range(1, group):
                    group_copy(k, g, lax.rem(r + group - g, group)).wait_recv()
                w_copy(half - 1 + k, w_slot(from_tp(k)), from_tp(k), pt).start()

        @pl.when(s >= d)
        def _(j=j):
            for h in range(heads):
                s_copy(j, h).wait_recv()
                if j + 1 == steps:
                    mine = excl[h]
                    got = last_recv_buf[h]
                    excl[h, :, width:] = split_mm(mine[:, :width], got) + mine[:, width:]
                    continue
                got = s_recv_buf[j, h]
                if j == 0:
                    excl[h] = got.astype(f32)
                else:
                    mine = excl[h]
                    new = split_mm(mine[:, :width], got)
                    excl[h] = jnp.concatenate(
                        [new[:, :width], new[:, width:] + mine[:, width:]], axis=1
                    )
                if j + 1 < steps:
                    mine = state[h]
                    new = split_mm(mine[:, :width], got)
                    state[h] = jnp.concatenate(
                        [new[:, :width], new[:, width:] + mine[:, width:]], axis=1
                    )

    def stage_two(i, carry):
        for h in range(heads):
            lanes = slice(h * width, (h + 1) * width)
            start = excl[h, :, width:].astype(bf16)
            raw = o_buf[fine(i), lanes] + mm(p_buf[fine(i), lanes], start)
            scale = lax.rsqrt(jnp.mean(raw * raw, axis=1, keepdims=True) + head_floor)
            place = pl.ds(pl.multiple_of(t * hw + h * width, width), width)
            heads_all[fine(i), place] = (raw * scale * hgain_ref[...]).astype(bf16)
        for k in range(1, half):
            h_copy(k, i, t, to_tp(k)).start()
        h_copy(0, i, t, pt).start()
        return carry

    lax.fori_loop(0, nh, stage_two, 0)
    for load in loads[2:]:
        load.wait()
    def relay_heads(i, carry):
        for k in range(1, half):
            h_copy(k, i, from_tp(k), pt).wait_recv()
            h_copy(half - 1 + k, i, from_tp(k), pt).start()
        return carry

    def rp_copy(slot, i, who):
        return remote(
            part_buf.at[fine(i), cols(who, cw)],
            rp_buf.at[slot, fine(i), :],
            rp_send.at[slot, i],
            rp_recv.at[slot, i],
            "tp",
            pt,
        )

    def rc_copy(k, i):
        return remote(
            cs_buf.at[k - 1, fine(i), :],
            cr_buf.at[k - 1, fine(i), :],
            rc_send.at[k - 1, i],
            rc_recv.at[k - 1, i],
            "tp",
            to_tp(k),
        )

    def pair_reduce(i):
        for k in range(1, half):
            rp_copy(k, i, pt).wait_recv()
            mine = part_buf[fine(i), cols(to_tp(k), cw)].astype(f32)
            cs_buf[k - 1, fine(i), :] = (mine + rp_buf[k, fine(i), :].astype(f32)).astype(bf16)
            rc_copy(k, i).start()

    relay_heads(0, 0)
    w_copy(0, w_slot(pt), pt, pt).wait_recv()
    for k in range(1, half):
        w_copy(half - 1 + k, w_slot(pair_tp(k)), pair_tp(k), pt).wait_recv()

    def stage_three(i, carry):
        h_copy(0, i, pt, pt).wait_recv()
        for k in range(1, half):
            h_copy(half - 1 + k, i, pair_tp(k), pt).wait_recv()
        res = x_full[fine(i), :].astype(f32) + mm(heads_all[fine(i), :], wo_full[...])
        res_tmp[...] = res

        @pl.when(i + 1 < nh)
        def _():
            relay_heads(i + 1, 0)

        @pl.when(i > 0)
        def _():
            pair_reduce(i - 1)

        res = res_tmp[...]
        scale = lax.rsqrt(jnp.mean(res * res, axis=1, keepdims=True) + norm_floor)
        normed = (res * scale * fgain_ref[...]).astype(bf16)
        gate = mm(normed, gate_w[...])
        up = mm(normed, up_w[...])
        hidden = (gate / (1.0 + jnp.exp(-gate)) * up).astype(bf16)
        part_buf[fine(i), :] = mm(hidden, down_w[...]).astype(bf16)
        for k in range(1, half):
            rp_copy(k, i, lax.rem(pt + 2 * k, n_tp)).start()
        rp_copy(0, i, pt).start()
        res_own[fine(i), :] = res_tmp[:, cols(t, cw)]

        return carry

    lax.fori_loop(0, nh, stage_three, 0)
    pair_reduce(nh - 1)

    def o_copy(i):
        return pltpu.make_async_copy(out_buf.at[fine(i), :], out_ref.at[fine(i), :], o_sem.at[i])

    def finish(i, carry):
        rp_copy(0, i, pt).wait_recv()
        total = res_own[fine(i), :] + part_buf[fine(i), cols(t, cw)].astype(f32)
        total = total + rp_buf[0, fine(i), :].astype(f32)
        for k in range(1, half):
            rc_copy(k, i).wait_recv()
            total = total + cr_buf[k - 1, fine(i), :].astype(f32)
        out_buf[fine(i), :] = total.astype(bf16)
        o_copy(i).start()
        return carry

    lax.fori_loop(0, nh, finish, 0)

    def drain(i, carry):
        for k in range(1, half):
            x_copy(k, i, x_hbm.at[rows(i), :], t, to_tp(k)).wait_send()
            x_copy(half - 1 + k, i, x_slot(i, from_tp(k)), from_tp(k), pt).wait_send()
        x_copy(0, i, x_hbm.at[rows(i), :], t, pt).wait_send()
        return carry

    def drain_fine(i, carry):
        for k in range(1, half):
            h_copy(k, i, t, to_tp(k)).wait_send()
            h_copy(half - 1 + k, i, from_tp(k), pt).wait_send()
            rp_copy(k, i, lax.rem(pt + 2 * k, n_tp)).wait_send()
            rc_copy(k, i).wait_send()
        h_copy(0, i, t, pt).wait_send()
        rp_copy(0, i, pt).wait_send()
        o_copy(i).wait()
        return carry

    lax.fori_loop(0, nc, drain, 0)
    lax.fori_loop(0, nh, drain_fine, 0)
    for k in range(1, half):
        part_copy(k, t, to_tp(k)).wait_send()
        for g in range(1, group):
            group_copy(k, g, r).wait_send()
        w_copy(half - 1 + k, w_slot(from_tp(k)), from_tp(k), pt).wait_send()
    w_copy(0, wo_hbm, t, pt).wait_send()
    for j in range(steps):

        @pl.when(s + 2**j < n_seq)
        def _(j=j):
            for h in range(heads):
                s_copy(j, h).wait_send()


def body(n_tp, n_seq, x, again, qkv, decay, rate, hgain, wo, fgain, gate, up, down):
    length, cw = x.shape
    width = hgain.shape[0]
    heads = qkv.shape[2] // width
    hw = heads * width
    full = cw * n_tp
    half = n_tp // 2
    span = 2 * width
    nc = length // span
    steps = (n_seq - 1).bit_length()
    slots = 2 * half - 1
    nh = length // width
    group = 4 if n_seq % 4 == 0 else 1
    anywhere = pl.BlockSpec(memory_space=pl.ANY)
    vmem = pl.BlockSpec(memory_space=pltpu.VMEM)
    dma = pltpu.SemaphoreType.DMA
    return pl.pallas_call(
        functools.partial(kernel, (n_tp, n_seq, span, width, steps, group)),
        out_shape=jax.ShapeDtypeStruct((length, cw), bf16),
        in_specs=[
            anywhere,
            vmem,
            anywhere,
            vmem,
            vmem,
            vmem,
            anywhere,
            vmem,
            anywhere,
            anywhere,
            anywhere,
        ],
        out_specs=anywhere,
        scratch_shapes=[
            pltpu.VMEM((length, full), bf16),
            pltpu.VMEM(qkv.shape, bf16),
            pltpu.VMEM(gate.shape, bf16),
            pltpu.VMEM(up.shape, bf16),
            pltpu.VMEM(down.shape, bf16),
            pltpu.VMEM((hw * n_tp, full), bf16),
            pltpu.VMEM((length, hw), f32),
            pltpu.VMEM((length, hw), bf16),
            pltpu.VMEM((length, hw * n_tp), bf16),
            pltpu.VMEM((heads, width, 2 * width), f32),
            pltpu.VMEM((heads, width, 2 * width), f32),
            pltpu.VMEM((steps, heads, width, 2 * width), bf16),
            pltpu.VMEM((steps, heads, width, 2 * width), bf16),
            pltpu.VMEM((heads, width, width), bf16),
            pltpu.VMEM((heads, width, width), bf16),
            pltpu.VMEM((width, full), f32),
            pltpu.VMEM((length, cw), f32),
            pltpu.VMEM((length, full), bf16),
            pltpu.VMEM((half, length, cw), bf16),
            pltpu.VMEM((half - 1, length, cw), bf16),
            pltpu.VMEM((half - 1, length, cw), bf16),
            pltpu.VMEM((length, cw), bf16),
            dma((6,)),
            dma((slots, nc)),
            dma((slots, nc)),
            dma((slots,)),
            dma((slots,)),
            dma((slots, nh)),
            dma((slots, nh)),
            dma((steps, heads)),
            dma((steps, heads)),
            dma((half, nh)),
            dma((half, nh)),
            dma((half - 1, nh)),
            dma((half - 1, nh)),
            dma((half - 1, group)),
            dma((half - 1, group)),
            dma((nh,)),
        ],
        compiler_params=pltpu.CompilerParams(
            collective_id=0, has_side_effects=True, vmem_limit_bytes=60 * 1024 * 1024
        ),
    )(
        x,
        again.reshape(1, full),
        qkv,
        decay,
        rate,
        hgain.reshape(1, width),
        wo,
        fgain.reshape(1, full),
        gate,
        up,
        down,
    )


def solution(mesh):
    placed = (
        P("seq", "tp"),
        P(),
        P(None, None, "tp"),
        P("tp", "seq"),
        P("tp", "seq"),
        P(),
        P("tp", None),
        P(),
        P(None, "tp"),
        P(None, "tp"),
        P("tp", None),
    )
    return jax.shard_map(
        functools.partial(body, mesh.shape["tp"], mesh.shape["seq"]),
        mesh=mesh,
        in_specs=placed,
        out_specs=P("seq", "tp"),
        check_vma=False,
    )
```

profile of v0, /device:TPU:27, one launch (start us, length us, event | category | flops | bytes accessed | tf_op | source)
XLA Modules:
  0.0 77.1 jit_solution(5850136669860963950)
XLA Ops:
  0.0 75.0 %shard_map.109 = bf16[768,512]{1,0:T(8,128)(2,1)} custom-call(bf16[768,512]{1,0:T(8,128)(2,1)} %x_hbm.1, f32[1,2048]{1,0:T(1,128)} %bitcast.3, bf16[3,2048,256]{2,1,0:T(8,128)(2,1)} %qkv_hbm.1, f32[2,768]{1,0:T(2,128)} %decay_ref.1, f32[2,768]{1,0:T(2,128)} %rate_ref.1, f32[1,128]{1,0:T(1,128)} %bitcast.5, bf16[256,2048]{1,0:T(8,128)(2,1)} %wo_hbm.1, ...), custom_call_target="tpu_custom_call" | custom-call | tf_op jit(solution)/shard_map/pallas_call | solution.py:519
  75.0 2.1 %copy.13 = bf16[768,512]{1,0:T(8,128)(2,1)} copy(bf16[768,512]{1,0:T(8,128)(2,1)} %shard_map.109) | data formatting | bytes 1572864
where the time goes:
time: 77.3 us; the launch traced here: 77.1 us
  Pallas kernels  75 us (97%)
  local copies, waits for them, and re-layouts  2.06 us (3%)
    pallas_call x1, Pallas kernels, body(): pl.pallas_call(functools.partial(kernel, (n_tp, n_seq, span, width, steps...  75 us
    unnamed x1, local copies, waits for them, and re-layouts  2.06 us

commit v1 on v0

--- a/solution.py
+++ b/solution.py
@@ -12,6 +12,10 @@
 bf16 = jnp.bfloat16
 f32 = jnp.float32
 MESH = pl.DeviceIdType.MESH
+SPAN = 2
+VL = 59
+EARLY = (0, 1, 1, 2)
+EARLY_TWIN = (2, 3, 3, 3)
 
 
 def mm(a, b):
@@ -71,12 +75,17 @@
     rp_buf,
     cs_buf,
     cr_buf,
-    out_buf,
     l_sem,
     x_send,
     x_recv,
     w_send,
     w_recv,
+    f_send,
+    f_recv,
+    q_send,
+    q_recv,
+    b_send,
+    b_recv,
     h_send,
     h_recv,
     s_send,
@@ -85,11 +94,8 @@
     rp_recv,
     rc_send,
     rc_recv,
-    g_send,
-    g_recv,
-    o_sem,
 ):
-    n_tp, n_seq, span, width, steps, group = cfg
+    n_tp, n_seq, span, width, steps, group, nb = cfg
     length, cw = x_hbm.shape
     heads = qkv_hbm.shape[2] // width
     hw = heads * width
@@ -98,12 +104,13 @@
     piece = width
     nh = length // piece
     share = hw // group
+    sub = share // nb
     subs = span // width
     t = lax.axis_index("tp")
     s = lax.axis_index("seq")
     pt = t + 1 - 2 * lax.rem(t, 2)
     r = lax.rem(s, group)
-    base = s - r
+    twin = s + 1 - 2 * r
 
     def to_tp(k):
         return lax.rem(t + 2 * k, n_tp)
@@ -132,11 +139,6 @@
 
         arrivals = arrivals + 1 - (s + d) // n_seq + (s + n_seq - d) // n_seq
 
-    for g in range(1, group):
-        other = base + lax.rem(r + g, group)
-        pl.semaphore_signal(barrier, inc=1, device_id={"seq": other}, device_id_type=MESH)
-        arrivals += 1
-
     def cols(j, w):
         return pl.ds(pl.multiple_of(j * w, w), w)
 
@@ -147,8 +149,8 @@
         return pl.ds(pl.multiple_of(i * piece, piece), piece)
 
     loads = [
+        pltpu.make_async_copy(x_hbm, x_full.at[:, cols(t, cw)], l_sem.at[1]),
         pltpu.make_async_copy(qkv_hbm, qkv_w, l_sem.at[0]),
-        pltpu.make_async_copy(x_hbm, x_full.at[:, cols(t, cw)], l_sem.at[1]),
         pltpu.make_async_copy(wo_hbm, wo_full.at[cols(t, hw), :], l_sem.at[2]),
         pltpu.make_async_copy(gate_hbm, gate_w, l_sem.at[3]),
         pltpu.make_async_copy(up_hbm, up_w, l_sem.at[4]),
@@ -157,6 +159,7 @@
     for load in loads[:2]:
         load.start()
     pl.semaphore_wait(barrier, arrivals)
+    loads[0].wait()
 
     def remote(src, dst, send, recv, axis, other):
         return pltpu.make_async_remote_copy(
@@ -185,37 +188,52 @@
     def w_slot(who):
         return wo_full.at[cols(who, hw), :]
 
-    def w_part(who, j):
-        return wo_full.at[pl.ds(pl.multiple_of(who * hw + j * share, share), share), :]
-
-    def part_copy(k, who, other):
-        src = wo_hbm.at[pl.ds(pl.multiple_of(r * share, share), share), :]
-        return remote(src, w_part(who, r), w_send.at[k], w_recv.at[k], "tp", other)
-
-    def group_copy(k, g, j):
-        slot = w_part(from_tp(k), j)
-        other = base + lax.rem(r + g, group)
-        return remote(slot, slot, g_send.at[k - 1, g], g_recv.at[k - 1, g], "seq", other)
+    def w_rows(k, j, b):
+        start = from_tp(k) * hw + j * share + b * sub
+        return wo_full.at[pl.ds(pl.multiple_of(start, sub), sub), :]
+
+    def pair_rows(k, j, b):
+        start = pair_tp(k) * hw + j * share + b * sub
+        return wo_full.at[pl.ds(pl.multiple_of(start, sub), sub), :]
+
+    def far_copy(k, b):
+        src = wo_hbm.at[pl.ds(pl.multiple_of(r * share + b * sub, sub), sub), :]
+        dst = wo_full.at[pl.ds(pl.multiple_of(t * hw + r * share + b * sub, sub), sub), :]
+        return remote(src, dst, f_send.at[k - 1, b], f_recv.at[k - 1, b], "tp", to_tp(k))
+
+    def twin_copy(k, b):
+        slot = w_rows(k, r, b)
+        return remote(slot, slot, q_send.at[k - 1, b], q_recv.at[k - 1, b], "seq", twin)
+
+    def pass_copy(k, g, j, b):
+        slot = w_rows(k, j, b)
+        return remote(slot, slot, b_send.at[k - 1, g, b], b_recv.at[k - 1, g, b], "tp", pt)
+
+    def spread(b):
+        for k in range(1, half):
+            far_copy(k, b).wait_recv()
+            if group > 1:
+                twin_copy(k, b).start()
+            pass_copy(k, 0, r, b).start()
+
+    def spread_twin(b):
+        for k in range(1, half):
+            if group > 1:
+                twin_copy(k, b).wait_recv()
+                pass_copy(k, 1, 1 - r, b).start()
 
     def w_copy(slot, src, who, other):
         return remote(src, w_slot(who), w_send.at[slot], w_recv.at[slot], "tp", other)
 
     def send_x(i, carry):
         for k in range(1, half):
-            x_copy(k, i, x_hbm.at[rows(i), :], t, to_tp(k)).start()
-        x_copy(0, i, x_hbm.at[rows(i), :], t, pt).start()
-
-        @pl.when(i == 0)
-        def _():
-            for k in range(1, half):
-                part_copy(k, t, to_tp(k)).start()
-
+            x_copy(k, i, x_slot(i, t), t, to_tp(k)).start()
+        x_copy(0, i, x_slot(i, t), t, pt).start()
         return carry
 
     lax.fori_loop(0, nc, send_x, 0)
     for load in loads[2:]:
         load.start()
-    loads[0].wait()
     loads[1].wait()
 
     row_id = lax.broadcasted_iota(jnp.int32, (width, width), 0)
@@ -232,11 +250,13 @@
 
         @pl.when(i == 1)
         def _():
-            for k in range(1, half):
-                part_copy(k, from_tp(k), pt).wait_recv()
-                for g in range(1, group):
-                    group_copy(k, g, r).start()
             w_copy(0, wo_hbm, t, pt).start()
+
+        @pl.when(i == nc - 2)
+        def _():
+            for b in range(nb):
+                for k in range(1, half):
+                    far_copy(k, b).start()
 
         x_copy(0, i, x_slot(i, pt), pt, pt).wait_recv()
         for k in range(1, half):
@@ -319,48 +339,62 @@
             src, dst = (last_send_buf.at[h], last_recv_buf.at[h])
         return remote(src, dst, s_send.at[j, h], s_recv.at[j, h], "seq", lax.rem(s + 2**j, n_seq))
 
+    def s_start(j, h):
+        @pl.when(s + 2**j < n_seq)
+        def _():
+            if j + 1 == steps:
+                last_send_buf[h] = state[h, :, width:].astype(bf16)
+            else:
+                s_send_buf[j, h] = state[h].astype(bf16)
+            s_copy(j, h).start()
+
+    early = [[] for _ in range(steps)]
+    early_twin = [[] for _ in range(steps)]
+    for b, j in enumerate(EARLY[:nb]):
+        if j < steps:
+            early[j].append(b)
+    for b, j in enumerate(EARLY_TWIN[:nb]):
+        if j < steps:
+            early_twin[j].append(b)
+
     for h in range(heads):
         excl[h] = jnp.concatenate([eye, jnp.zeros((width, width), f32)], axis=1)
+        if steps > 0:
+            s_start(0, h)
     for j in range(steps):
-        d = 2**j
-
-        @pl.when(s + d < n_seq)
-        def _(j=j):
-            if j + 1 == steps:
-                last_send_buf[...] = state[:, :, width:].astype(bf16)
-            else:
-                s_send_buf[j] = state[...].astype(bf16)
-            for h in range(heads):
-                s_copy(j, h).start()
-
-        if j == 0:
-            for k in range(1, half):
-                for g in range(1, group):
-                    group_copy(k, g, lax.rem(r + group - g, group)).wait_recv()
-                w_copy(half - 1 + k, w_slot(from_tp(k)), from_tp(k), pt).start()
-
-        @pl.when(s >= d)
-        def _(j=j):
-            for h in range(heads):
+        for b in early[j]:
+            spread(b)
+        for b in early_twin[j]:
+            spread_twin(b)
+        for h in range(heads):
+
+            @pl.when(s >= 2**j)
+            def _(j=j, h=h):
                 s_copy(j, h).wait_recv()
                 if j + 1 == steps:
                     mine = excl[h]
                     got = last_recv_buf[h]
                     excl[h, :, width:] = split_mm(mine[:, :width], got) + mine[:, width:]
-                    continue
+                    return
                 got = s_recv_buf[j, h]
-                if j == 0:
-                    excl[h] = got.astype(f32)
-                else:
+                mine = state[h]
+                new = split_mm(mine[:, :width], got)
+                state[h] = jnp.concatenate(
+                    [new[:, :width], new[:, width:] + mine[:, width:]], axis=1
+                )
+
+            if j + 1 < steps:
+                s_start(j + 1, h)
+
+                @pl.when(s >= 2**j)
+                def _(j=j, h=h):
+                    got = s_recv_buf[j, h]
+                    if j == 0:
+                        excl[h] = got.astype(f32)
+                        return
                     mine = excl[h]
                     new = split_mm(mine[:, :width], got)
                     excl[h] = jnp.concatenate(
-                        [new[:, :width], new[:, width:] + mine[:, width:]], axis=1
-                    )
-                if j + 1 < steps:
-                    mine = state[h]
-                    new = split_mm(mine[:, :width], got)
-                    state[h] = jnp.concatenate(
                         [new[:, :width], new[:, width:] + mine[:, width:]], axis=1
                     )
 
@@ -378,6 +412,12 @@
         return carry
 
     lax.fori_loop(0, nh, stage_two, 0)
+    for b in range(nb):
+        if not any(b in some for some in early):
+            spread(b)
+    for b in range(nb):
+        if not any(b in some for some in early_twin):
+            spread_twin(b)
     for load in loads[2:]:
         load.wait()
     def relay_heads(i, carry):
@@ -416,7 +456,12 @@
     relay_heads(0, 0)
     w_copy(0, w_slot(pt), pt, pt).wait_recv()
     for k in range(1, half):
-        w_copy(half - 1 + k, w_slot(pair_tp(k)), pair_tp(k), pt).wait_recv()
+        for b in range(nb):
+            for g in range(group):
+                slot = pair_rows(k, r + g * (1 - 2 * r), b)
+                remote(
+                    slot, slot, b_send.at[k - 1, g, b], b_recv.at[k - 1, g, b], "tp", pt
+                ).wait_recv()
 
     def stage_three(i, carry):
         h_copy(0, i, pt, pt).wait_recv()
@@ -450,9 +495,6 @@
     lax.fori_loop(0, nh, stage_three, 0)
     pair_reduce(nh - 1)
 
-    def o_copy(i):
-        return pltpu.make_async_copy(out_buf.at[fine(i), :], out_ref.at[fine(i), :], o_sem.at[i])
-
     def finish(i, carry):
         rp_copy(0, i, pt).wait_recv()
         total = res_own[fine(i), :] + part_buf[fine(i), cols(t, cw)].astype(f32)
@@ -460,17 +502,16 @@
         for k in range(1, half):
             rc_copy(k, i).wait_recv()
             total = total + cr_buf[k - 1, fine(i), :].astype(f32)
-        out_buf[fine(i), :] = total.astype(bf16)
-        o_copy(i).start()
+        out_ref[fine(i), :] = total.astype(bf16)
         return carry
 
     lax.fori_loop(0, nh, finish, 0)
 
     def drain(i, carry):
         for k in range(1, half):
-            x_copy(k, i, x_hbm.at[rows(i), :], t, to_tp(k)).wait_send()
+            x_copy(k, i, x_slot(i, t), t, to_tp(k)).wait_send()
             x_copy(half - 1 + k, i, x_slot(i, from_tp(k)), from_tp(k), pt).wait_send()
-        x_copy(0, i, x_hbm.at[rows(i), :], t, pt).wait_send()
+        x_copy(0, i, x_slot(i, t), t, pt).wait_send()
         return carry
 
     def drain_fine(i, carry):
@@ -481,16 +522,17 @@
             rc_copy(k, i).wait_send()
         h_copy(0, i, t, pt).wait_send()
         rp_copy(0, i, pt).wait_send()
-        o_copy(i).wait()
         return carry
 
     lax.fori_loop(0, nc, drain, 0)
     lax.fori_loop(0, nh, drain_fine, 0)
     for k in range(1, half):
-        part_copy(k, t, to_tp(k)).wait_send()
-        for g in range(1, group):
-            group_copy(k, g, r).wait_send()
-        w_copy(half - 1 + k, w_slot(from_tp(k)), from_tp(k), pt).wait_send()
+        for b in range(nb):
+            far_copy(k, b).wait_send()
+            if group > 1:
+                twin_copy(k, b).wait_send()
+            for g in range(group):
+                pass_copy(k, g, r + g * (1 - 2 * r), b).wait_send()
     w_copy(0, wo_hbm, t, pt).wait_send()
     for j in range(steps):
 
@@ -507,18 +549,19 @@
     hw = heads * width
     full = cw * n_tp
     half = n_tp // 2
-    span = 2 * width
+    span = SPAN * width
     nc = length // span
     steps = (n_seq - 1).bit_length()
     slots = 2 * half - 1
     nh = length // width
-    group = 4 if n_seq % 4 == 0 else 1
+    group = 2 if n_seq % 2 == 0 else 1
+    nb = 4
     anywhere = pl.BlockSpec(memory_space=pl.ANY)
     vmem = pl.BlockSpec(memory_space=pltpu.VMEM)
     dma = pltpu.SemaphoreType.DMA
     return pl.pallas_call(
-        functools.partial(kernel, (n_tp, n_seq, span, width, steps, group)),
-        out_shape=jax.ShapeDtypeStruct((length, cw), bf16),
+        functools.partial(kernel, (n_tp, n_seq, span, width, steps, group, nb)),
+        out_shape=pltpu.VMEM((length, cw), bf16),
         in_specs=[
             anywhere,
             vmem,
@@ -532,7 +575,7 @@
             anywhere,
             anywhere,
         ],
-        out_specs=anywhere,
+        out_specs=pl.BlockSpec(memory_space=pltpu.VMEM),
         scratch_shapes=[
             pltpu.VMEM((length, full), bf16),
             pltpu.VMEM(qkv.shape, bf16),
@@ -555,12 +598,17 @@
             pltpu.VMEM((half, length, cw), bf16),
             pltpu.VMEM((half - 1, length, cw), bf16),
             pltpu.VMEM((half - 1, length, cw), bf16),
-            pltpu.VMEM((length, cw), bf16),
             dma((6,)),
             dma((slots, nc)),
             dma((slots, nc)),
-            dma((slots,)),
-            dma((slots,)),
+            dma((1,)),
+            dma((1,)),
+            dma((half - 1, nb)),
+            dma((half - 1, nb)),
+            dma((half - 1, nb)),
+            dma((half - 1, nb)),
+            dma((half - 1, group, nb)),
+            dma((half - 1, group, nb)),
             dma((slots, nh)),
             dma((slots, nh)),
             dma((steps, heads)),
@@ -569,12 +617,9 @@
             dma((half, nh)),
             dma((half - 1, nh)),
             dma((half - 1, nh)),
-            dma((half - 1, group)),
-            dma((half - 1, group)),
-            dma((nh,)),
         ],
         compiler_params=pltpu.CompilerParams(
-            collective_id=0, has_side_effects=True, vmem_limit_bytes=60 * 1024 * 1024
+            collective_id=0, has_side_effects=True, vmem_limit_bytes=VL * 1024 * 1024
         ),
     )(
         x,

time: 77.3 us -> 70.2 us (0.908)
  the two profiles are of different devices: /device:TPU:27 before, /device:TPU:9 now
where the time goes in v1:
time: 70.2 us; the launch traced here: 69.3 us
  Pallas kernels  68.5 us (98%)
  local copies, waits for them, and re-layouts  0.88 us (1%)
    pallas_call x1, Pallas kernels, body(): pl.pallas_call(functools.partial(kernel, (n_tp, n_seq, span, width, steps...  68.5 us

profile of v1, /device:TPU:9, one launch (start us, length us, event | category | flops | bytes accessed | tf_op | source)
XLA Modules:
  0.0 69.3 jit_solution(656362291995652256)
XLA Ops:
  0.0 68.5 %shard_map.109 = bf16[768,512]{1,0:T(8,128)(2,1)S(1)} custom-call(bf16[768,512]{1,0:T(8,128)(2,1)} %x_hbm.1, f32[1,2048]{1,0:T(1,128)} %bitcast.3, bf16[3,2048,256]{2,1,0:T(8,128)(2,1)} %qkv_hbm.1, f32[2,768]{1,0:T(2,128)} %decay_ref.1, f32[2,768]{1,0:T(2,128)} %rate_ref.1, f32[1,128]{1,0:T(1,128)} %bitcast.5, bf16[256,2048]{1,0:T(8,128)(2,1)} %wo_hbm.1, ...), custom_call_target="tpu_custom_call" | custom-call | tf_op jit(solution)/shard_map/pallas_call | solution.py:562
  68.5 0.9 %copy.13 = bf16[768,512]{1,0:T(8,128)(2,1)} copy(bf16[768,512]{1,0:T(8,128)(2,1)S(1)} %shard_map.109) | data formatting | bytes 1572864

commit v2 on v1

v2 whole, which is shorter than its diff:
```python
import functools

import jax
import jax.numpy as jnp
from jax import lax
from jax.experimental import pallas as pl
from jax.experimental.pallas import tpu as pltpu
from jax.sharding import PartitionSpec as P

norm_floor = 0.1
head_floor = 0.05
bf16 = jnp.bfloat16
f32 = jnp.float32
MESH = pl.DeviceIdType.MESH
VL = 59
XG = 1
FAR = 2
EARLY = (0, 1, 2, 2)
EARLY_TWIN = (2, 3, 3, 3)


def mm(a, b):
    return jnp.dot(a, b, preferred_element_type=f32)


def mm_nt(a, b):
    return lax.dot_general(a, b, (((1,), (1,)), ((), ())), preferred_element_type=f32)


def mm_tn(a, b):
    return lax.dot_general(a, b, (((0,), (0,)), ((), ())), preferred_element_type=f32)


def split_mm(a, b):
    high = a.astype(bf16)
    low = (a - high.astype(f32)).astype(bf16)
    return mm(high, b) + mm(low, b)


def unit_rows(u):
    return u * lax.rsqrt(jnp.sum(u * u, axis=-1, keepdims=True) + 1.0)


def kernel(
    cfg,
    x_hbm,
    again_hbm,
    qkv_hbm,
    decay_hbm,
    rate_hbm,
    hgain_hbm,
    wo_hbm,
    fgain_hbm,
    gate_hbm,
    up_hbm,
    down_hbm,
    out_ref,
    again_ref,
    decay_ref,
    rate_ref,
    hgain_ref,
    fgain_ref,
    below_buf,
    upto_buf,
    rate_buf,
    growth_buf,
    grown_buf,
    tail_buf,
    last_buf,
    x_full,
    qkv_w,
    gate_w,
    up_w,
    down_w,
    wo_full,
    o_buf,
    p_buf,
    heads_all,
    state,
    excl,
    s_send_buf,
    s_recv_buf,
    last_send_buf,
    last_recv_buf,
    heads_own,
    res_tmp,
    base_buf,
    pair_buf,
    part_buf,
    cr_buf,
    l_sem,
    x_send,
    x_recv,
    w_send,
    w_recv,
    f_send,
    f_recv,
    q_send,
    q_recv,
    b_send,
    b_recv,
    h_send,
    h_recv,
    s_send,
    s_recv,
    e_send,
    e_recv,
    rp_send,
    rp_recv,
    rc_send,
    rc_recv,
):
    n_tp, n_seq, span, width, steps, group, nb = cfg
    length, cw = x_hbm.shape
    full = cw * n_tp
    parts = 4
    heads = qkv_hbm.shape[2] // width
    hw = heads * width
    half = n_tp // 2
    nc = length // span
    piece = width
    nh = length // piece
    mine = nh // 2
    hidden_w = gate_hbm.shape[1]
    share = hw // group
    sub = share // nb
    t = lax.axis_index("tp")
    s = lax.axis_index("seq")
    c = lax.rem(t, 2)
    chip = t // 2
    pt = t + 1 - 2 * c
    r = lax.rem(s, group)
    twin = s + 1 - 2 * r

    def to_tp(k):
        return lax.rem(t + 2 * k, n_tp)

    def from_tp(k):
        return lax.rem(t + n_tp - 2 * k, n_tp)

    def pair_tp(k):
        return lax.rem(pt + n_tp - 2 * k, n_tp)

    def cross(k, e):
        return lax.rem(chip + k, half) * 2 + e

    def crossed(k, e):
        return lax.rem(chip + half - k, half) * 2 + e

    barrier = pltpu.get_barrier_semaphore()
    arrivals = 0
    for other in [pt] + [cross(k, e) for k in range(1, half) for e in range(2)]:
        pl.semaphore_signal(barrier, inc=1, device_id={"tp": other}, device_id_type=MESH)
        arrivals += 1
    for j in range(steps):
        d = 2**j

        @pl.when(s + d < n_seq)
        def _(d=d):
            pl.semaphore_signal(barrier, inc=1, device_id={"seq": s + d}, device_id_type=MESH)

        @pl.when(s >= d)
        def _(d=d):
            pl.semaphore_signal(barrier, inc=1, device_id={"seq": s - d}, device_id_type=MESH)

        arrivals = arrivals + 1 - (s + d) // n_seq + (s + n_seq - d) // n_seq

    def cols(j, w):
        return pl.ds(pl.multiple_of(j * w, w), w)

    def rows(i):
        return pl.ds(pl.multiple_of(i * span, span), span)

    def fine(i):
        return pl.ds(pl.multiple_of(i * piece, piece), piece)

    loads = [
        pltpu.make_async_copy(x_hbm, x_full.at[:, cols(t, cw)], l_sem.at[1]),
        pltpu.make_async_copy(qkv_hbm, qkv_w, l_sem.at[0]),
        pltpu.make_async_copy(wo_hbm, wo_full.at[cols(t, hw), :], l_sem.at[2]),
        pltpu.make_async_copy(gate_hbm, gate_w.at[:, cols(c, hidden_w)], l_sem.at[3]),
        pltpu.make_async_copy(up_hbm, up_w.at[:, cols(c, hidden_w)], l_sem.at[4]),
        pltpu.make_async_copy(down_hbm, down_w.at[cols(c, hidden_w), :], l_sem.at[5]),
    ]
    small = [
        pltpu.make_async_copy(src, dst, l_sem.at[6 + n])
        for n, (src, dst) in enumerate(
            (
                (again_hbm, again_ref),
                (decay_hbm, decay_ref),
                (rate_hbm, rate_ref),
                (hgain_hbm, hgain_ref),
                (fgain_hbm, fgain_ref),
            )
        )
    ]
    loads[0].start()
    for load in small:
        load.start()
    loads[1].start()
    pl.semaphore_wait(barrier, arrivals)
    loads[0].wait()

    def remote(src, dst, send, recv, axis, other):
        return pltpu.make_async_remote_copy(
            src_ref=src,
            dst_ref=dst,
            send_sem=send,
            recv_sem=recv,
            device_id={axis: other},
            device_id_type=MESH,
        )

    def x_slot(i, who):
        return x_full.at[rows(i), cols(who, cw)]

    def x_copy(slot, i, src, who, other):
        return remote(src, x_slot(i, who), x_send.at[slot, i], x_recv.at[slot, i], "tp", other)

    def h_slot(i, who):
        return heads_all.at[fine(i), cols(who, hw)]

    def h_copy(k, i):
        e = lax.rem(i, 2)
        slot, other = (0, pt) if k == 0 else (1 + (k - 1) * 2 + c, cross(k, e))
        return remote(
            heads_own.at[fine(i), :],
            h_slot(i // 2, t),
            h_send.at[k, i],
            h_recv.at[slot, i // 2],
            "tp",
            other,
        )

    def h_wait(i):
        for k in range(half):
            for e in range(2 if k > 0 else 1):
                who, slot = (pt, 0) if k == 0 else (crossed(k, e), 1 + (k - 1) * 2 + e)
                remote(
                    heads_own.at[fine(i), :],
                    h_slot(i, who),
                    h_send.at[k, i],
                    h_recv.at[slot, i],
                    "tp",
                    who,
                ).wait_recv()

    def e_copy(n, i, who):
        if n == 2:
            size = hidden_w // parts
            at = pl.ds(pl.multiple_of(i * size, size), size)
            dst = down_w.at[pl.ds(pl.multiple_of(who * hidden_w + i * size, size), size), :]
            src = down_hbm.at[at, :]
        else:
            size = full // parts
            at = pl.ds(pl.multiple_of(i * size, size), size)
            dst = (gate_w, up_w)[n].at[at, cols(who, hidden_w)]
            src = (gate_hbm, up_hbm)[n].at[at, :]
        return remote(src, dst, e_send.at[n, i], e_recv.at[n, i], "tp", pt)

    def share_weights(first, stop):
        for i in range(first, stop):
            for n in range(3):
                e_copy(n, i, c).start()

    def w_slot(who):
        return wo_full.at[cols(who, hw), :]

    def w_rows(k, j, b):
        start = from_tp(k) * hw + j * share + b * sub
        return wo_full.at[pl.ds(pl.multiple_of(start, sub), sub), :]

    def pair_rows(k, j, b):
        start = pair_tp(k) * hw + j * share + b * sub
        return wo_full.at[pl.ds(pl.multiple_of(start, sub), sub), :]

    def far_copy(k, b):
        src = wo_hbm.at[pl.ds(pl.multiple_of(r * share + b * sub, sub), sub), :]
        dst = wo_full.at[pl.ds(pl.multiple_of(t * hw + r * share + b * sub, sub), sub), :]
        return remote(src, dst, f_send.at[k - 1, b], f_recv.at[k - 1, b], "tp", to_tp(k))

    def twin_copy(k, b):
        slot = w_rows(k, r, b)
        return remote(slot, slot, q_send.at[k - 1, b], q_recv.at[k - 1, b], "seq", twin)

    def pass_copy(k, g, j, b):
        slot = w_rows(k, j, b)
        return remote(slot, slot, b_send.at[k - 1, g, b], b_recv.at[k - 1, g, b], "tp", pt)

    def spread(b):
        for k in range(1, half):
            far_copy(k, b).wait_recv()
            if group > 1:
                twin_copy(k, b).start()
            pass_copy(k, 0, r, b).start()

    def spread_twin(b):
        for k in range(1, half):
            if group > 1:
                twin_copy(k, b).wait_recv()
                pass_copy(k, 1, 1 - r, b).start()

    def w_copy(slot, src, who, other):
        return remote(src, w_slot(who), w_send.at[slot], w_recv.at[slot], "tp", other)

    def send_x(i, carry):
        for k in range(1, half):
            x_copy(k, i, x_slot(i, t), t, to_tp(k)).start()
        x_copy(0, i, x_slot(i, t), t, pt).start()
        return carry

    lax.fori_loop(0, nc, send_x, 0)
    for load in loads[2:]:
        load.start()
    w_copy(0, wo_hbm, t, pt).start()
    share_weights(0, parts // 2)
    for load in small:
        load.wait()

    row_id = lax.broadcasted_iota(jnp.int32, (width, width), 0)
    col_id = lax.broadcasted_iota(jnp.int32, (width, width), 1)
    eye = (row_id == col_id).astype(f32)
    upto = (row_id <= col_id).astype(f32)
    for h in range(heads):
        state[h] = jnp.concatenate([eye, jnp.zeros((width, width), f32)], axis=1)

    xor = row_id ^ col_id

    def fold_gain(i, carry):
        at = cols(i, width)
        gain = jnp.broadcast_to(again_ref[:, at], (width, width)).T
        gain = jnp.concatenate([gain] * heads, axis=1)
        for j in range(3):
            qkv_w[j, at, :] = (qkv_w[j, at, :].astype(f32) * gain).astype(bf16)
        return carry

    def prepare(i, carry):
        at = fine(i)
        lanes = cols(i, width)
        cumul = jnp.dot(
            decay_ref[:, lanes], upto, precision=lax.Precision.HIGHEST, preferred_element_type=f32
        )
        rate = rate_ref[:, lanes]
        for h in range(heads):
            c_row = jnp.broadcast_to(cumul[h : h + 1, :], (width, width))
            c_col = c_row.T
            b_col = jnp.broadcast_to(rate[h : h + 1, :], (width, width)).T
            c_end = cumul[h : h + 1, width - 1 : width]
            weights = jnp.exp(jnp.minimum(c_col - c_row, 0.0))
            growth = jnp.exp(c_col)
            below_buf[h, at, :] = jnp.where(row_id > col_id, b_col * weights, 0.0)
            upto_buf[h, at, :] = jnp.where(row_id >= col_id, weights, 0.0)
            rate_buf[h, at, :] = b_col
            growth_buf[h, at, :] = growth
            grown_buf[h, at, :] = b_col * growth
            tail_buf[h, at, :] = jnp.exp(c_end - c_col)
            last_buf[i, h : h + 1, :] = jnp.broadcast_to(jnp.exp(c_end), (1, 2 * width))
        return carry

    lax.fori_loop(0, nh, prepare, 0)
    loads[1].wait()
    lax.fori_loop(0, full // width, fold_gain, 0)

    def gather(i):
        for k in range(1, half):
            x_copy(k, i, x_slot(i, from_tp(k)), from_tp(k), pt).wait_recv()
            x_copy(half - 1 + k, i, x_slot(i, from_tp(k)), from_tp(k), pt).start()

    def gathered(i):
        x_copy(0, i, x_slot(i, pt), pt, pt).wait_recv()
        for k in range(1, half):
            x_copy(half - 1 + k, i, x_slot(i, pair_tp(k)), pair_tp(k), pt).wait_recv()

    def invert(lower):
        chains = list(lower)
        inverse = {cell: eye - jnp.where(xor < 2, lower[cell], 0.0) for cell in chains}
        block = 2
        while block < width:
            merge = 4 if 4 * block <= width else 2
            now = (xor >= block) & (xor < merge * block)
            small = {cell: inverse[cell].astype(bf16) for cell in chains}
            off = {
                cell: mm(small[cell], jnp.where(now, lower[cell], 0.0).astype(bf16)).astype(bf16)
                for cell in chains
            }
            inverse = {cell: inverse[cell] - mm(off[cell], small[cell]) for cell in chains}
            if merge == 4:
                square = {cell: mm(off[cell], off[cell]).astype(bf16) for cell in chains}
                inverse = {
                    cell: inverse[cell] + mm(square[cell], inverse[cell].astype(bf16))
                    for cell in chains
                }
            block *= merge
        return inverse

    def chunk(first, subs, between=None):
        span = subs * width
        here = pl.ds(pl.multiple_of(first, width), span)
        x = x_full[here, :]
        wide = x.astype(f32)
        scale = lax.rsqrt(jnp.mean(wide * wide, axis=1, keepdims=True) + norm_floor)
        k_all = mm(x, qkv_w[1]) * scale
        v_all = mm(x, qkv_w[2]) * scale
        q_all = mm(x, qkv_w[0]) * scale
        chains = [(c, h) for c in range(subs) for h in range(heads)]
        lower, mixing, right, tail, growth_q, last = {}, {}, {}, {}, {}, {}
        for c in range(subs):
            at = pl.ds(pl.multiple_of(first + c * width, width), width)
            for h in range(heads):
                cell = (c, h)
                part = (slice(c * width, (c + 1) * width), slice(h * width, (h + 1) * width))
                q = unit_rows(q_all[part])
                k = unit_rows(k_all[part])
                kb = k.astype(bf16)
                both = mm_nt(jnp.concatenate([kb, q.astype(bf16)], axis=0), kb)
                lower[cell] = both[:width] * below_buf[h, at, :]
                mixing[cell] = (both[width:] * upto_buf[h, at, :]).astype(bf16)
                right[cell] = jnp.concatenate(
                    [rate_buf[h, at, :] * v_all[part], grown_buf[h, at, :] * k], axis=1
                ).astype(bf16)
                tail[cell] = (k * tail_buf[h, at, :]).astype(bf16)
                growth_q[cell] = growth_buf[h, at, :] * q
                last[cell] = last_buf[first // width + c, h : h + 1, :]
        inverse = invert(lower)
        solved = {cell: mm(inverse[cell].astype(bf16), right[cell]).astype(bf16) for cell in chains}
        moved = {cell: mm_tn(tail[cell], solved[cell]) for cell in chains}
        before_b = {}
        for c in range(subs):
            for h in range(heads):
                cell = (c, h)
                before = state[h]
                before_b[cell] = before.astype(bf16)
                change = mm(moved[cell][:, width:].astype(bf16), before_b[cell])
                after = last[cell] * before - change
                state[h] = jnp.concatenate(
                    [after[:, :width], after[:, width:] + moved[cell][:, :width]], axis=1
                )
        if between is not None:
            between()
        mixed = {cell: mm(mixing[cell], solved[cell]) for cell in chains}
        for c in range(subs):
            at = pl.ds(pl.multiple_of(first + c * width, width), width)
            for h in range(heads):
                cell = (c, h)
                lanes = slice(h * width, (h + 1) * width)
                entry = (growth_q[cell] - mixed[cell][:, width:]).astype(bf16)
                entered = mm(entry, before_b[cell])
                p_buf[at, lanes] = entered[:, :width].astype(bf16)
                o_buf[at, lanes] = mixed[cell][:, :width] + entered[:, width:]

    def s_copy(j, h):
        src, dst = (s_send_buf.at[j, h], s_recv_buf.at[j, h])
        if j + 1 == steps:
            src, dst = (last_send_buf.at[h], last_recv_buf.at[h])
        return remote(src, dst, s_send.at[j, h], s_recv.at[j, h], "seq", lax.rem(s + 2**j, n_seq))

    def s_start(j, h):
        @pl.when(s + 2**j < n_seq)
        def _():
            if j + 1 == steps:
                last_send_buf[h] = state[h, :, width:].astype(bf16)
            else:
                s_send_buf[j, h] = state[h].astype(bf16)
            s_copy(j, h).start()

    early = [[] for _ in range(steps)]
    early_twin = [[] for _ in range(steps)]
    for b, j in enumerate(EARLY[:nb]):
        if j < steps:
            early[j].append(b)
    for b, j in enumerate(EARLY_TWIN[:nb]):
        if j < steps:
            early_twin[j].append(b)

    subs = 2 if nh % 2 == 0 else 1
    per = subs * width // span
    big = nh // subs

    def stage_one(i, carry):
        for n in range(1, per):
            gather(per * i + n)

        @pl.when(i == FAR)
        def _():
            for b in range(nb):
                for k in range(1, half):
                    far_copy(k, b).start()
            share_weights(parts // 2, parts)

        for n in range(per):
            gathered(per * i + n)

        def between():
            @pl.when(i + 1 < big)
            def _():
                gather(per * (i + 1))

            @pl.when(i + 1 == big)
            def _():
                for h in range(heads):
                    excl[h] = jnp.concatenate([eye, jnp.zeros((width, width), f32)], axis=1)
                    if steps > 0:
                        s_start(0, h)

        chunk(i * subs * width, subs, between)
        return carry

    gather(0)
    lax.fori_loop(0, big, stage_one, 0)
    for j in range(steps):
        for b in early[j]:
            spread(b)
        for b in early_twin[j]:
            spread_twin(b)
        for h in range(heads):

            @pl.when(s >= 2**j)
            def _(j=j, h=h):
                s_copy(j, h).wait_recv()
                if j + 1 == steps:
                    mine = excl[h]
                    got = last_recv_buf[h]
                    excl[h, :, width:] = split_mm(mine[:, :width], got) + mine[:, width:]
                    return
                got = s_recv_buf[j, h]
                mine = state[h]
                new = split_mm(mine[:, :width], got)
                state[h] = jnp.concatenate(
                    [new[:, :width], new[:, width:] + mine[:, width:]], axis=1
                )

            if j + 1 < steps:
                s_start(j + 1, h)

                @pl.when(s >= 2**j)
                def _(j=j, h=h):
                    got = s_recv_buf[j, h]
                    if j == 0:
                        excl[h] = got.astype(f32)
                        return
                    mine = excl[h]
                    new = split_mm(mine[:, :width], got)
                    excl[h] = jnp.concatenate(
                        [new[:, :width], new[:, width:] + mine[:, width:]], axis=1
                    )

    def stage_two(i, carry):
        for h in range(heads):
            lanes = slice(h * width, (h + 1) * width)
            start = excl[h, :, width:].astype(bf16)
            raw = o_buf[fine(i), lanes] + mm(p_buf[fine(i), lanes], start)
            scale = lax.rsqrt(jnp.mean(raw * raw, axis=1, keepdims=True) + head_floor)
            heads_own[fine(i), lanes] = (raw * scale * hgain_ref[...]).astype(bf16)
        for k in range(1, half):
            h_copy(k, i).start()

        @pl.when(lax.rem(i, 2) != c)
        def _():
            h_copy(0, i).start()

        @pl.when(lax.rem(i, 2) == c)
        def _():
            heads_all[fine(i // 2), cols(t, hw)] = heads_own[fine(i), :]

        return carry

    lax.fori_loop(0, nh, stage_two, 0)
    for b in range(nb):
        if not any(b in some for some in early):
            spread(b)
    for b in range(nb):
        if not any(b in some for some in early_twin):
            spread_twin(b)
    for load in loads[2:]:
        load.wait()
    for i in range(parts):
        for n in range(3):
            e_copy(n, i, 1 - c).wait_recv()

    def base_copy(i):
        return remote(
            pair_buf.at[fine(i), :],
            base_buf.at[fine(2 * i + c), :],
            rp_send.at[i],
            rp_recv.at[i],
            "tp",
            pt,
        )

    def rc_copy(k, e, i):
        p = 2 * i + c
        return remote(
            part_buf.at[fine(i), cols(cross(k, e), cw)],
            cr_buf.at[k - 1, fine(p), :],
            rc_send.at[k - 1, e, i],
            rc_recv.at[k - 1, p],
            "tp",
            cross(k, e),
        )

    w_copy(0, w_slot(pt), pt, pt).wait_recv()
    for k in range(1, half):
        for b in range(nb):
            for g in range(group):
                slot = pair_rows(k, r + g * (1 - 2 * r), b)
                remote(
                    slot, slot, b_send.at[k - 1, g, b], b_recv.at[k - 1, g, b], "tp", pt
                ).wait_recv()

    def stage_three(i, carry):
        p = 2 * i + c
        h_wait(i)
        res = x_full[fine(p), :].astype(f32) + mm(heads_all[fine(i), :], wo_full[...])
        scale = lax.rsqrt(jnp.mean(res * res, axis=1, keepdims=True) + norm_floor)
        res_tmp[...] = res
        normed = (res * scale * fgain_ref[...]).astype(bf16)
        gate = mm(normed, gate_w[...])
        up = mm(normed, up_w[...])
        hidden = (gate / (1.0 + jnp.exp(-gate)) * up).astype(bf16)
        part = mm(hidden, down_w[...])
        part_buf[fine(i), :] = part.astype(bf16)
        for k in range(1, half):
            for e in range(2):
                rc_copy(k, e, i).start()
        res_tmp[...] = res_tmp[...] + part
        pair_buf[fine(i), :] = res_tmp[:, cols(pt, cw)]
        base_copy(i).start()
        base_buf[fine(p), :] = res_tmp[:, cols(t, cw)]
        return carry

    lax.fori_loop(0, mine, stage_three, 0)

    def finish(p, carry):
        @pl.when(lax.rem(p, 2) != c)
        def _():
            remote(
                pair_buf.at[fine(p // 2), :],
                base_buf.at[fine(p), :],
                rp_send.at[p // 2],
                rp_recv.at[p // 2],
                "tp",
                pt,
            ).wait_recv()

        total = base_buf[fine(p), :]
        for k in range(1, half):
            remote(
                part_buf.at[fine(p // 2), cols(t, cw)],
                cr_buf.at[k - 1, fine(p), :],
                rc_send.at[k - 1, 0, p // 2],
                rc_recv.at[k - 1, p],
                "tp",
                crossed(k, lax.rem(p, 2)),
            ).wait_recv()
            total = total + cr_buf[k - 1, fine(p), :].astype(f32)
        out_ref[fine(p), :] = total.astype(bf16)
        return carry

    lax.fori_loop(0, nh, finish, 0)

    def drain(i, carry):
        for k in range(1, half):
            x_copy(k, i, x_slot(i, t), t, to_tp(k)).wait_send()
            x_copy(half - 1 + k, i, x_slot(i, from_tp(k)), from_tp(k), pt).wait_send()
        x_copy(0, i, x_slot(i, t), t, pt).wait_send()
        return carry

    def drain_heads(i, carry):
        for k in range(1, half):
            h_copy(k, i).wait_send()

        @pl.when(lax.rem(i, 2) != c)
        def _():
            h_copy(0, i).wait_send()

        return carry

    def drain_fine(i, carry):
        for k in range(1, half):
            for e in range(2):
                rc_copy(k, e, i).wait_send()
        base_copy(i).wait_send()
        return carry

    lax.fori_loop(0, nc, drain, 0)
    lax.fori_loop(0, nh, drain_heads, 0)
    lax.fori_loop(0, mine, drain_fine, 0)
    for i in range(parts):
        for n in range(3):
            e_copy(n, i, c).wait_send()
    for k in range(1, half):
        for b in range(nb):
            far_copy(k, b).wait_send()
            if group > 1:
                twin_copy(k, b).wait_send()
            for g in range(group):
                pass_copy(k, g, r + g * (1 - 2 * r), b).wait_send()
    w_copy(0, wo_hbm, t, pt).wait_send()
    for j in range(steps):

        @pl.when(s + 2**j < n_seq)
        def _(j=j):
            for h in range(heads):
                s_copy(j, h).wait_send()


def body(n_tp, n_seq, x, again, qkv, decay, rate, hgain, wo, fgain, gate, up, down):
    length, cw = x.shape
    width = hgain.shape[0]
    heads = qkv.shape[2] // width
    hw = heads * width
    full = cw * n_tp
    parts = 4
    half = n_tp // 2
    span = XG * width
    nc = length // span
    steps = (n_seq - 1).bit_length()
    slots = 2 * half - 1
    nh = length // width
    group = 2 if n_seq % 2 == 0 else 1
    nb = 4
    anywhere = pl.BlockSpec(memory_space=pl.ANY)
    dma = pltpu.SemaphoreType.DMA
    return pl.pallas_call(
        functools.partial(kernel, (n_tp, n_seq, span, width, steps, group, nb)),
        out_shape=pltpu.VMEM((length, cw), bf16),
        in_specs=[anywhere] * 11,
        out_specs=pl.BlockSpec(memory_space=pltpu.VMEM),
        scratch_shapes=[
            pltpu.VMEM((1, full), f32),
            pltpu.VMEM(decay.shape, f32),
            pltpu.VMEM(rate.shape, f32),
            pltpu.VMEM((1, width), f32),
            pltpu.VMEM((1, full), f32),
            *[pltpu.VMEM((heads, length, width), f32)] * 6,
            pltpu.VMEM((nh, heads, 2 * width), f32),
            pltpu.VMEM((length, full), bf16),
            pltpu.VMEM(qkv.shape, bf16),
            pltpu.VMEM((full, 2 * gate.shape[1]), bf16),
            pltpu.VMEM((full, 2 * up.shape[1]), bf16),
            pltpu.VMEM((2 * down.shape[0], full), bf16),
            pltpu.VMEM((hw * n_tp, full), bf16),
            pltpu.VMEM((length, hw), f32),
            pltpu.VMEM((length, hw), bf16),
            pltpu.VMEM((length // 2, hw * n_tp), bf16),
            pltpu.VMEM((heads, width, 2 * width), f32),
            pltpu.VMEM((heads, width, 2 * width), f32),
            pltpu.VMEM((steps, heads, width, 2 * width), bf16),
            pltpu.VMEM((steps, heads, width, 2 * width), bf16),
            pltpu.VMEM((heads, width, width), bf16),
            pltpu.VMEM((heads, width, width), bf16),
            pltpu.VMEM((length, hw), bf16),
            pltpu.VMEM((width, full), f32),
            pltpu.VMEM((length, cw), f32),
            pltpu.VMEM((length // 2, cw), f32),
            pltpu.VMEM((length // 2, full), bf16),
            pltpu.VMEM((half - 1, length, cw), bf16),
            dma((11,)),
            dma((slots, nc)),
            dma((slots, nc)),
            dma((1,)),
            dma((1,)),
            dma((half - 1, nb)),
            dma((half - 1, nb)),
            dma((half - 1, nb)),
            dma((half - 1, nb)),
            dma((half - 1, group, nb)),
            dma((half - 1, group, nb)),
            dma((half, nh)),
            dma((slots, nh // 2)),
            dma((steps, heads)),
            dma((steps, heads)),
            dma((3, parts)),
            dma((3, parts)),
            dma((nh // 2,)),
            dma((nh // 2,)),
            dma((half - 1, 2, nh // 2)),
            dma((half - 1, nh)),
        ],
        compiler_params=pltpu.CompilerParams(
            collective_id=0, has_side_effects=True, vmem_limit_bytes=VL * 1024 * 1024
        ),
    )(
        x,
        again.reshape(1, full),
        qkv,
        decay,
        rate,
        hgain.reshape(1, width),
        wo,
        fgain.reshape(1, full),
        gate,
        up,
        down,
    )


def solution(mesh):
    placed = (
        P("seq", "tp"),
        P(),
        P(None, None, "tp"),
        P("tp", "seq"),
        P("tp", "seq"),
        P(),
        P("tp", None),
        P(),
        P(None, "tp"),
        P(None, "tp"),
        P("tp", None),
    )
    return jax.shard_map(
        functools.partial(body, mesh.shape["tp"], mesh.shape["seq"]),
        mesh=mesh,
        in_specs=placed,
        out_specs=P("seq", "tp"),
        check_vma=False,
    )
```

time: 70.2 us -> 67.2 us (0.957); the launches traced: 69.3 us -> 67.1 us
  Pallas kernels: 68.5 us -> 66.2 us
    pallas_call x1, Pallas kernels: 68.5 us -> 66.2 us  [body(): pl.pallas_call(functools.partial(kernel, (n_tp, n_seq, span, width, steps...]
where the time goes in v2:
time: 67.2 us; the launch traced here: 67.1 us
  Pallas kernels  66.2 us (99%)
  local copies, waits for them, and re-layouts  0.88 us (1%)
    pallas_call x1, Pallas kernels, body(): pl.pallas_call(functools.partial(kernel, (n_tp, n_seq, span, width, steps...  66.2 us

profile of v2, /device:TPU:9, one launch (start us, length us, event | category | flops | bytes accessed | tf_op | source)
XLA Modules:
  0.0 67.1 jit_solution(15300965265961843304)
XLA Ops:
  0.0 66.2 %shard_map.109 = bf16[768,512]{1,0:T(8,128)(2,1)S(1)} custom-call(bf16[768,512]{1,0:T(8,128)(2,1)} %x_hbm.1, f32[1,2048]{1,0:T(1,128)} %bitcast.3, bf16[3,2048,256]{2,1,0:T(8,128)(2,1)} %qkv_hbm.1, f32[2,768]{1,0:T(2,128)} %decay_hbm.1, f32[2,768]{1,0:T(2,128)} %rate_hbm.1, f32[1,128]{1,0:T(1,128)} %bitcast.5, bf16[256,2048]{1,0:T(8,128)(2,1)} %wo_hbm.1, ...), custom_call_target="tpu_custom_call" | custom-call | tf_op jit(solution)/shard_map/pallas_call | solution.py:724
  66.2 0.9 %copy.13 = bf16[768,512]{1,0:T(8,128)(2,1)} copy(bf16[768,512]{1,0:T(8,128)(2,1)S(1)} %shard_map.109) | data formatting | bytes 1572864

commit v3 on v2

--- a/solution.py
+++ b/solution.py
@@ -16,7 +16,7 @@
 XG = 1
 FAR = 2
 EARLY = (0, 1, 2, 2)
-EARLY_TWIN = (2, 3, 3, 3)
+EARLY_TWIN = (2, 2, 3, 3)
 
 
 def mm(a, b):
@@ -67,6 +67,8 @@
     grown_buf,
     tail_buf,
     last_buf,
+    early_buf,
+    square_buf,
     x_full,
     qkv_w,
     gate_w,
@@ -367,11 +369,10 @@
             x_copy(half - 1 + k, i, x_slot(i, from_tp(k)), from_tp(k), pt).start()
 
     def gathered(i):
-        x_copy(0, i, x_slot(i, pt), pt, pt).wait_recv()
         for k in range(1, half):
             x_copy(half - 1 + k, i, x_slot(i, pair_tp(k)), pair_tp(k), pt).wait_recv()
 
-    def invert(lower):
+    def solve(lower, right):
         chains = list(lower)
         inverse = {cell: eye - jnp.where(xor < 2, lower[cell], 0.0) for cell in chains}
         block = 2
@@ -383,6 +384,10 @@
                 cell: mm(small[cell], jnp.where(now, lower[cell], 0.0).astype(bf16)).astype(bf16)
                 for cell in chains
             }
+            block *= merge
+            if block == width:
+                inverse = {cell: mm(small[cell], right[cell]) for cell in chains}
+                small = {cell: inverse[cell].astype(bf16) for cell in chains}
             inverse = {cell: inverse[cell] - mm(off[cell], small[cell]) for cell in chains}
             if merge == 4:
                 square = {cell: mm(off[cell], off[cell]).astype(bf16) for cell in chains}
@@ -390,18 +395,23 @@
                     cell: inverse[cell] + mm(square[cell], inverse[cell].astype(bf16))
                     for cell in chains
                 }
-            block *= merge
         return inverse
 
     def chunk(first, subs, between=None):
         span = subs * width
         here = pl.ds(pl.multiple_of(first, width), span)
-        x = x_full[here, :]
-        wide = x.astype(f32)
-        scale = lax.rsqrt(jnp.mean(wide * wide, axis=1, keepdims=True) + norm_floor)
-        k_all = mm(x, qkv_w[1]) * scale
-        v_all = mm(x, qkv_w[2]) * scale
-        q_all = mm(x, qkv_w[0]) * scale
+        square = square_buf[here, :1]
+        q_all, k_all, v_all = [early_buf[n, here, :] for n in range(3)]
+        for n in range(1, half):
+            at = cols(pair_tp(n), cw)
+            x = x_full[here, at]
+            wide = x.astype(f32)
+            square = square + jnp.sum(wide * wide, axis=1, keepdims=True)
+            k_all = k_all + mm(x, qkv_w[1, at, :])
+            v_all = v_all + mm(x, qkv_w[2, at, :])
+            q_all = q_all + mm(x, qkv_w[0, at, :])
+        scale = lax.rsqrt(square * (1.0 / full) + norm_floor)
+        q_all, k_all, v_all = q_all * scale, k_all * scale, v_all * scale
         chains = [(c, h) for c in range(subs) for h in range(heads)]
         lower, mixing, right, tail, growth_q, last = {}, {}, {}, {}, {}, {}
         for c in range(subs):
@@ -421,8 +431,8 @@
                 tail[cell] = (k * tail_buf[h, at, :]).astype(bf16)
                 growth_q[cell] = growth_buf[h, at, :] * q
                 last[cell] = last_buf[first // width + c, h : h + 1, :]
-        inverse = invert(lower)
-        solved = {cell: mm(inverse[cell].astype(bf16), right[cell]).astype(bf16) for cell in chains}
+        answer = solve(lower, right)
+        solved = {cell: answer[cell].astype(bf16) for cell in chains}
         moved = {cell: mm_tn(tail[cell], solved[cell]) for cell in chains}
         before_b = {}
         for c in range(subs):
@@ -487,6 +497,16 @@
                     far_copy(k, b).start()
             share_weights(parts // 2, parts)
 
+        here = pl.ds(pl.multiple_of(i * subs * width, subs * width), subs * width)
+        for k in range(1, half):
+            at = cols(from_tp(k), cw)
+            x = x_full[here, at]
+            wide = x.astype(f32)
+            square_buf[here, :] += jnp.broadcast_to(
+                jnp.sum(wide * wide, axis=1, keepdims=True), (subs * width, width)
+            )
+            for n in range(3):
+                early_buf[n, here, :] += mm(x, qkv_w[n, at, :])
         for n in range(per):
             gathered(per * i + n)
 
@@ -505,6 +525,20 @@
         chunk(i * subs * width, subs, between)
         return carry
 
+    def stage_zero(i, carry):
+        for n in range(per):
+            x_copy(0, per * i + n, x_slot(per * i + n, pt), pt, pt).wait_recv()
+        at = cols(chip, 2 * cw)
+        here = pl.ds(pl.multiple_of(i * subs * width, subs * width), subs * width)
+        x = x_full[here, at]
+        wide = x.astype(f32)
+        square = jnp.sum(wide * wide, axis=1, keepdims=True)
+        square_buf[here, :] = jnp.broadcast_to(square, (subs * width, width))
+        for n in range(3):
+            early_buf[n, here, :] = mm(x, qkv_w[n, at, :])
+        return carry
+
+    lax.fori_loop(0, big, stage_zero, 0)
     gather(0)
     lax.fori_loop(0, big, stage_one, 0)
     for j in range(steps):
@@ -734,6 +768,8 @@
             pltpu.VMEM((1, full), f32),
             *[pltpu.VMEM((heads, length, width), f32)] * 6,
             pltpu.VMEM((nh, heads, 2 * width), f32),
+            pltpu.VMEM((3, length, hw), f32),
+            pltpu.VMEM((length, width), f32),
             pltpu.VMEM((length, full), bf16),
             pltpu.VMEM(qkv.shape, bf16),
             pltpu.VMEM((full, 2 * gate.shape[1]), bf16),

time: 67.2 us -> 66.6 us (level)
  Pallas kernels: 66.2 us -> 65.5 us
where the time goes in v3:
time: 66.6 us; the launch traced here: 66.4 us
  Pallas kernels  65.5 us (98%)
  local copies, waits for them, and re-layouts  0.88 us (1%)
    pallas_call x1, Pallas kernels, body(): pl.pallas_call(functools.partial(kernel, (n_tp, n_seq, span, width, steps...  65.5 us

profile of v3, /device:TPU:9, one launch (start us, length us, event | category | flops | bytes accessed | tf_op | source)
XLA Modules:
  0.0 66.4 jit_solution(16290184848704945703)
XLA Ops:
  0.0 65.5 %shard_map.109 = bf16[768,512]{1,0:T(8,128)(2,1)S(1)} custom-call(bf16[768,512]{1,0:T(8,128)(2,1)} %x_hbm.1, f32[1,2048]{1,0:T(1,128)} %bitcast.3, bf16[3,2048,256]{2,1,0:T(8,128)(2,1)} %qkv_hbm.1, f32[2,768]{1,0:T(2,128)} %decay_hbm.1, f32[2,768]{1,0:T(2,128)} %rate_hbm.1, f32[1,128]{1,0:T(1,128)} %bitcast.5, bf16[256,2048]{1,0:T(8,128)(2,1)} %wo_hbm.1, ...), custom_call_target="tpu_custom_call" | custom-call | tf_op jit(solution)/shard_map/pallas_call | solution.py:758
  65.5 0.9 %copy.13 = bf16[768,512]{1,0:T(8,128)(2,1)} copy(bf16[768,512]{1,0:T(8,128)(2,1)S(1)} %shard_map.109) | data formatting | bytes 1572864

commit v4 on v3

--- a/solution.py
+++ b/solution.py
@@ -69,6 +69,7 @@
     last_buf,
     early_buf,
     square_buf,
+    own_buf,
     x_full,
     qkv_w,
     gate_w,
@@ -234,8 +235,8 @@
             other,
         )
 
-    def h_wait(i):
-        for k in range(half):
+    def h_wait(i, some):
+        for k in some:
             for e in range(2 if k > 0 else 1):
                 who, slot = (pt, 0) if k == 0 else (crossed(k, e), 1 + (k - 1) * 2 + e)
                 remote(
@@ -599,13 +600,24 @@
         return carry
 
     lax.fori_loop(0, nh, stage_two, 0)
+    loads[2].wait()
+    w_copy(0, w_slot(pt), pt, pt).wait_recv()
+
+    def own_part(i, carry):
+        h_wait(i, range(1))
+        at = cols(chip, 2 * hw)
+        x = x_full[fine(2 * i + c), :].astype(f32)
+        own_buf[fine(i), :] = x + mm(heads_all[fine(i), at], wo_full[at, :])
+        return carry
+
+    lax.fori_loop(0, mine, own_part, 0)
     for b in range(nb):
         if not any(b in some for some in early):
             spread(b)
     for b in range(nb):
         if not any(b in some for some in early_twin):
             spread_twin(b)
-    for load in loads[2:]:
+    for load in loads[3:]:
         load.wait()
     for i in range(parts):
         for n in range(3):
@@ -632,7 +644,7 @@
             cross(k, e),
         )
 
-    w_copy(0, w_slot(pt), pt, pt).wait_recv()
+
     for k in range(1, half):
         for b in range(nb):
             for g in range(group):
@@ -643,8 +655,11 @@
 
     def stage_three(i, carry):
         p = 2 * i + c
-        h_wait(i)
-        res = x_full[fine(p), :].astype(f32) + mm(heads_all[fine(i), :], wo_full[...])
+        h_wait(i, range(1, half))
+        res = own_buf[fine(i), :]
+        for n in range(1, half):
+            at = cols(lax.rem(chip + n, half), 2 * hw)
+            res = res + mm(heads_all[fine(i), at], wo_full[at, :])
         scale = lax.rsqrt(jnp.mean(res * res, axis=1, keepdims=True) + norm_floor)
         res_tmp[...] = res
         normed = (res * scale * fgain_ref[...]).astype(bf16)
@@ -770,6 +785,7 @@
             pltpu.VMEM((nh, heads, 2 * width), f32),
             pltpu.VMEM((3, length, hw), f32),
             pltpu.VMEM((length, width), f32),
+            pltpu.VMEM((length // 2, full), f32),
             pltpu.VMEM((length, full), bf16),
             pltpu.VMEM(qkv.shape, bf16),
             pltpu.VMEM((full, 2 * gate.shape[1]), bf16),

time: 66.6 us -> 66.3 us (level)
  no operation moved by 1% of the time
where the time goes in v4:
time: 66.3 us; the launch traced here: 66.1 us
  Pallas kernels  65.2 us (98%)
  local copies, waits for them, and re-layouts  0.88 us (1%)
    pallas_call x1, Pallas kernels, body(): pl.pallas_call(functools.partial(kernel, (n_tp, n_seq, span, width, steps...  65.2 us

profile of v4, /device:TPU:9, one launch (start us, length us, event | category | flops | bytes accessed | tf_op | source)
XLA Modules:
  0.0 66.1 jit_solution(341651552517451648)
XLA Ops:
  0.0 65.2 %shard_map.109 = bf16[768,512]{1,0:T(8,128)(2,1)S(1)} custom-call(bf16[768,512]{1,0:T(8,128)(2,1)} %x_hbm.1, f32[1,2048]{1,0:T(1,128)} %bitcast.3, bf16[3,2048,256]{2,1,0:T(8,128)(2,1)} %qkv_hbm.1, f32[2,768]{1,0:T(2,128)} %decay_hbm.1, f32[2,768]{1,0:T(2,128)} %rate_hbm.1, f32[1,128]{1,0:T(1,128)} %bitcast.5, bf16[256,2048]{1,0:T(8,128)(2,1)} %wo_hbm.1, ...), custom_call_target="tpu_custom_call" | custom-call | tf_op jit(solution)/shard_map/pallas_call | solution.py:773
  65.2 0.9 %copy.13 = bf16[768,512]{1,0:T(8,128)(2,1)} copy(bf16[768,512]{1,0:T(8,128)(2,1)S(1)} %shard_map.109) | data formatting | bytes 1572864
